TPU v7x, 512 devices: a whole 4x4x16 slice. The times are simulated.
512 devices in a mesh: obs: 16 (over z_hi, y, core), flux: 32 (over z_lo, x).
Axes of the slice: x: 4, y: 4, z: 16 (z_hi: 2, z_lo: 8; z = z_hi * 8 + z_lo), core: 2. Of those that a mesh axis runs over, the one named last changes fastest.
Arguments:
- jacobian: bfloat16 [2048, 32768], P('obs', 'flux'), may hold values from -0.03125 to 0.03125
- probes: bfloat16 [2, 32768, 128], P(None, 'flux'), may hold values from -6 to 6
- prior_std: float32 [32768], P('flux'), may hold values from 0.5 to 2
- obs_weight: float32 [2048], P('obs'), may hold values from 0.25 to 4
Outputs:
- sketch: float32 [32768, 256], P(('flux', 'obs'))
- basis_out: float32 [32768, 256], P(('flux', 'obs'))
All inputs are finite; a program needn't handle non-finite values.
Results may differ from a plain program's by a relative error of at most 0.005.
Values may be sent and summed in bfloat16 or wider, within the bound.
No kernel may reach another device: no remote copies, remote signals or barrier semaphores. Data moves between devices by JAX's collectives and lax.ppermute only.
A program may use at most 64 MiB of HBM per device.

v0:
```python
import math

import jax
import jax.numpy as jnp
from jax import lax
from jax.sharding import PartitionSpec as P


def body(jacobian, probes, prior_std, obs_weight):
    block_count, flux_local, probe_count = probes.shape
    scaled = (probes.astype(jnp.float32) * prior_std[None, :, None]).astype(jnp.bfloat16)
    portion = flux_local // lax.axis_size("obs")
    offset = lax.axis_index("obs") * portion
    local_std = lax.dynamic_slice_in_dim(prior_std, offset, portion)
    stacked = jnp.transpose(scaled, (1, 0, 2)).reshape(flux_local, block_count * probe_count)
    forward = lax.psum(jnp.dot(jacobian, stacked, preferred_element_type=jnp.float32), "flux")
    weighted = (forward * obs_weight[:, None]).astype(jnp.bfloat16)
    adjoint = lax.psum_scatter(
        lax.dot_general(
            jacobian, weighted, (((0,), (0,)), ((), ())), preferred_element_type=jnp.float32
        ),
        "obs",
        scatter_dimension=0,
        tiled=True,
    )
    sketch = adjoint * local_std[:, None]
    gram_matrix = lax.psum(
        jnp.dot(
            sketch.T, sketch, precision=lax.Precision.HIGHEST, preferred_element_type=jnp.float32
        ),
        ("obs", "flux"),
    )
    factor = jnp.linalg.cholesky(gram_matrix)
    scale_root = math.sqrt(flux_local * lax.axis_size("flux"))
    basis_out = jax.scipy.linalg.solve_triangular(factor, sketch.T, lower=True).T * scale_root
    return (sketch, basis_out)


def solution(mesh):
    in_specs = (P("obs", "flux"), P(None, "flux", None), P("flux"), P("obs"))
    out_specs = (P(("flux", "obs"), None), P(("flux", "obs"), None))
    return jax.shard_map(body, mesh=mesh, in_specs=in_specs, out_specs=out_specs, check_vma=False)
```

profile of v0, /device:TPU:1, one launch (start us, length us, event | category | flops | bytes accessed | tf_op | source)
XLA Modules:
  0.0 1084.4 jit_solution(11429978422342303576)
XLA Ops:
  7.2 0.0 copy-start
  7.2 0.0 copy-start.4
  7.2 0.0 all-reduce.4.cloned.1.call-start
  7.2 1.3 copy.13
  8.5 0.0 copy-done.4
  8.5 0.1 multiply_convert_fusion
  8.6 0.0 copy-done
  8.7 1.0 convolution_bitcast_fusion.1
  9.6 0.0 copy-start.5
  9.6 0.0 all-reduce.4.cloned.1.call-update
  9.6 0.0 reduce-scatter.4.cloned.1.call-start
  9.7 419.5 %all-reduce.4.cloned.1.call-done = f32[128,256]{0,1:T(8,128)} async-done(((f32[128,256]{0,1:T(8,128)}), f32[128,256]{0,1:T(8,128)}) %all-reduce.4.cloned.1.call-update) | async-done | bytes 131088 | tf_op jit(solution)/shard_map/psum | solution.py:16
  429.2 0.0 copy-done.5
  429.2 1.2 convolution_bitcast_fusion
  430.4 1.3 copy.18
  431.7 0.0 reduce-scatter.4.cloned.1.call-update
  431.7 0.0 all-reduce.6.cloned.1.call-start
  431.8 0.1 dynamic_slice.3
  431.9 121.9 %reduce-scatter.4.cloned.1.call-done = f32[64,256]{1,0:T(8,128)} async-done(((f32[1024,256]{1,0:T(8,128)}), f32[64,256]{1,0:T(8,128)}) %reduce-scatter.4.cloned.1.call-update) | async-done | bytes 65552 | tf_op jit(solution)/shard_map/reduce_scatter | solution.py:18
  553.8 0.9 broadcast_multiply_fusion
  554.7 0.0 copy-start.2
  554.7 1.1 fusion.11
  555.8 0.0 copy-done.2
  555.8 0.0 copy-start.3
  555.8 0.0 all-reduce.6.cloned.1.call-update
  555.8 0.8 copy-done.3
  556.6 0.1 fusion.21
  556.7 459.3 %all-reduce.6.cloned.1.call-done = f32[256,256]{0,1:T(8,128)} async-done(((f32[256,256]{0,1:T(8,128)}), f32[256,256]{0,1:T(8,128)}) %all-reduce.6.cloned.1.call-update) | async-done | bytes 262160 | tf_op jit(solution)/shard_map/psum | solution.py:27
  1016.0 0.0 copy-start.1
  1016.0 1.1 copy.16
  1017.1 0.0 copy-done.1
  1017.2 11.7 %cholesky.50 = f32[128,128]{1,0:T(8,128)S(1)} custom-call(f32[128,128]{1,0:T(8,128)S(1)} %cholesky.118), custom_call_target="Cholesky" | custom-call | tf_op jit(solution)/shard_map/jit(cholesky)/cholesky | solution.py:33
  1029.0 9.8 custom-call.15
  1038.8 0.2 constant_dynamic-update-slice_fusion.1
  1039.0 0.3 convolution_subtract_fusion
  1039.3 11.7 %cholesky.105 = f32[128,128]{1,0:T(8,128)S(1)} custom-call(f32[128,128]{1,0:T(8,128)S(1)} %convolution_subtract_fusion), custom_call_target="Cholesky" | custom-call | tf_op jit(solution)/shard_map/jit(cholesky)/cholesky | solution.py:33
  1051.0 0.7 compare_reduce_fusion
  1052.9 0.1 triangular_solve.57
  1053.0 3.9 while.1
  1053.2 0.6 fusion.23
  1053.7 1.3 bitcast_dynamic-update-slice_fusion.2
  1055.0 0.6 fusion.23
  1055.6 1.3 bitcast_dynamic-update-slice_fusion.2
  1056.9 19.7 %custom-call.16 = f32[2,128,128]{1,2,0:T(8,128)S(1)} custom-call(f32[2,128,128]{2,1,0:T(8,128)S(1)} %get-tuple-element.9), custom_call_target="InvertDiagBlocksLowerTriangular" | custom-call | tf_op jit(solution)/shard_map/jit(_solve_triangular)/triangular_solve | solution.py:35
  1076.6 0.2 fusion.3
  1076.8 0.2 convolution_subtract_fusion.1
  1077.0 0.2 fusion.2
  1077.2 0.6 fusion.6
  (10 shorter events, 0.2 us)
Async XLA Ops:
  7.2 1.5 copy-start
  7.2 1.3 copy-start.4
  7.2 422.0 %all-reduce.4.cloned.1.call-start = ((), (), s32[]{:S(2)}) async-start(), calls=%async_computation.1 | async-start | bytes 262144 | tf_op jit(solution)/shard_map/psum | solution.py:16
  9.6 419.6 %copy-start.5 = (f32[128]{0:T(128)S(1)}, f32[128]{0:T(128)}, u32[]{:S(2)}) copy-start(f32[128]{0:T(128)} %param.7) | copy-start | bytes 1540
  9.6 544.1 %reduce-scatter.4.cloned.1.call-start = ((), (), s32[]{:S(2)}) async-start(), calls=%async_computation.3 | async-start | bytes 1114112 | tf_op jit(solution)/shard_map/reduce_scatter | solution.py:18
  431.7 584.2 %all-reduce.6.cloned.1.call-start = ((), (), s32[]{:S(2)}) async-start(), calls=%async_computation.2 | async-start | bytes 524288 | tf_op jit(solution)/shard_map/psum | solution.py:27
  554.7 1.1 copy-start.2
  555.8 0.8 copy-start.3
  1016.0 1.2 copy-start.1
Sparse Core Ops, SparseCore 0:
  10.9 418.2 all-reduce.3
  433.9 119.8 reduce-scatter.3
  559.2 456.7 all-reduce.5
where the time goes:
time: 1090 us; the launch traced here: 1080 us
  waiting for transfers between devices  1000 us (92%)
  other arithmetic  55.4 us (5%)
  between operations  15.1 us (1%)
    psum x1, waiting for transfers between devices, body(): lax.psum(jnp.dot(sketch.T, sketch, precision=lax.Precision.HIGHEST, prefe...  459 us
    psum x1, waiting for transfers between devices, body(): lax.psum(jnp.dot(jacobian, stacked, preferred_element_type=jnp.float32),...  420 us
    reduce_scatter x1, waiting for transfers between devices, body(): lax.psum_scatter(lax.dot_general(jacobian, weighted, (((0,), (0,)), ((),...  122 us
    another operation x6, other arithmetic, body(): factor = jnp.linalg.cholesky(gram_matrix)  34 us
  transfers between devices with their start and end apart: 3, of which 3 were waited for; matrix products, arithmetic and copies ran while one was open for 0% of the time, Pallas kernels for 0%

commit v1 on v0

v1 whole, which is shorter than its diff:
```python
import math

import jax
import jax.numpy as jnp
from jax import lax
from jax.sharding import Mesh, PartitionSpec as P

OBS_AXES = ("zh", "y", "c")
FLUX_AXES = ("zl", "x")
PLANE = ("y", "c", "x")
LINE = ("zh", "zl")


def scatter_sum(parts, axes):
    moved = lax.all_to_all(parts, axes, 0, 0, tiled=True)
    return jnp.sum(moved.astype(jnp.float32), axis=0)


def gather(piece, axes):
    count = lax.axis_size(axes)
    return lax.all_to_all(
        jnp.broadcast_to(piece[None], (count, *piece.shape)), axes, 0, 0, tiled=True
    )


def to_tiles(full):
    rows, cols = full.shape
    return full.reshape(rows // 8, 8, cols // 128, 128).transpose(0, 2, 1, 3).reshape(-1, 8, 128)


def from_tiles(tiles, rows, cols):
    return tiles.reshape(rows // 8, cols // 128, 8, 128).transpose(0, 2, 1, 3).reshape(rows, cols)


def body(jacobian, probes, prior_std, obs_weight):
    block_count, flux_local, probe_count = probes.shape
    obs_local = jacobian.shape[0]
    columns = block_count * probe_count
    obs_parts = lax.axis_size(OBS_AXES)
    scaled = (probes.astype(jnp.float32) * prior_std[None, :, None]).astype(jnp.bfloat16)
    stacked = jnp.transpose(scaled, (1, 0, 2)).reshape(flux_local, columns)
    partial = jnp.dot(jacobian, stacked, preferred_element_type=jnp.float32)
    tile = scatter_sum(to_tiles(partial), FLUX_AXES)
    row = lax.axis_index(FLUX_AXES) // (columns // 128) * 8
    weight = lax.dynamic_slice_in_dim(obs_weight, row, 8)
    weighted = from_tiles(
        gather((tile * weight[:, None]).astype(jnp.bfloat16), FLUX_AXES), obs_local, columns
    )
    adjoint = lax.dot_general(
        jacobian, weighted, (((0,), (0,)), ((), ())), preferred_element_type=jnp.float32
    ).astype(jnp.bfloat16)
    portion = flux_local // obs_parts
    adjoint = scatter_sum(adjoint.reshape(obs_parts, portion, columns), OBS_AXES)
    local_std = lax.dynamic_slice_in_dim(prior_std, lax.axis_index(OBS_AXES) * portion, portion)
    sketch = adjoint * local_std[:, None]
    gram = jnp.dot(
        sketch.T, sketch, precision=lax.Precision.HIGHEST, preferred_element_type=jnp.float32
    )
    slab = scatter_sum(gram.reshape(lax.axis_size(PLANE), -1, columns), PLANE)
    slab = jnp.sum(gather(slab, LINE), axis=0)
    gram = gather(slab, PLANE).reshape(columns, columns)
    factor = jnp.linalg.cholesky(gram)
    scale_root = math.sqrt(flux_local * lax.axis_size(FLUX_AXES))
    basis_out = jax.scipy.linalg.solve_triangular(factor, sketch.T, lower=True).T * scale_root
    return (sketch, basis_out)


def solution(mesh):
    split = Mesh(mesh.devices.reshape(2, 4, 2, 8, 4), ("zh", "y", "c", "zl", "x"))
    in_specs = (P(OBS_AXES, FLUX_AXES), P(None, FLUX_AXES, None), P(FLUX_AXES), P(OBS_AXES))
    out_specs = (P(FLUX_AXES + OBS_AXES, None), P(FLUX_AXES + OBS_AXES, None))
    return jax.shard_map(
        body, mesh=split, in_specs=in_specs, out_specs=out_specs, check_vma=False
    )
```

time: 1090 us -> 205 us (0.19)
  waiting for transfers between devices: 1000 us -> 46.2 us
  blocking collectives: 0 us -> 54.3 us
  starting transfers between devices: 0.12 us -> 35.4 us
  between operations: 15.1 us -> 2.14 us
    psum x2 -> x0, waiting for transfers between devices: 879 us -> none  [the longest x1 459 us: body(): lax.psum(jnp.dot(sketch.T, sketch, precision=lax.Precision.HIGHEST, prefe...]
    reduce_scatter x1 -> x0, waiting for transfers between devices: 122 us -> none  [body(): lax.psum_scatter(lax.dot_general(jacobian, weighted, (((0,), (0,)), ((),...]
    all_to_all x0 -> x3, blocking collectives: none -> 54.3 us  [the longest x2 39.5 us: gather(): lax.all_to_all(jnp.broadcast_to(piece[None], (count, *piece.shape)), axes...]
    all_to_all x0 -> x3, waiting for transfers between devices: none -> 46.2 us  [the longest x2 37.4 us: scatter_sum(): moved = lax.all_to_all(parts, axes, 0, 0, tiled=True)]
    all_to_all x0 -> x3, starting transfers between devices: none -> 35.4 us  [the longest x2 28.6 us: scatter_sum(): moved = lax.all_to_all(parts, axes, 0, 0, tiled=True)]
where the time goes in v1:
time: 205 us; the launch traced here: 204 us
  other arithmetic  55.1 us (27%)
  blocking collectives  54.3 us (26%)
  waiting for transfers between devices  46.2 us (23%)
  starting transfers between devices  35.4 us (17%)
  local copies, waits for them, and re-layouts  9.03 us (4%)
  between operations  2.14 us (1%)
  matrix products  2.11 us (1%)
    all_to_all x2, blocking collectives, gather(): lax.all_to_all(jnp.broadcast_to(piece[None], (count, *piece.shape)), axes...  39.5 us
    all_to_all x2, waiting for transfers between devices, scatter_sum(): moved = lax.all_to_all(parts, axes, 0, 0, tiled=True)  37.4 us
    another operation x6, other arithmetic, body(): factor = jnp.linalg.cholesky(gram)  34 us
    all_to_all x2, starting transfers between devices, scatter_sum(): moved = lax.all_to_all(parts, axes, 0, 0, tiled=True)  28.6 us
    another operation x3, other arithmetic, body(): jax.scipy.linalg.solve_triangular(factor, sketch.T, lower=True)  19.9 us
    all_to_all x1, blocking collectives, scatter_sum(): moved = lax.all_to_all(parts, axes, 0, 0, tiled=True)  14.8 us
    all_to_all x1, waiting for transfers between devices, gather(): lax.all_to_all(jnp.broadcast_to(piece[None], (count, *piece.shape)), axes...  8.77 us
    all_to_all x1, starting transfers between devices, gather(): lax.all_to_all(jnp.broadcast_to(piece[None], (count, *piece.shape)), axes...  6.79 us
  transfers between devices with their start and end apart: 3, of which 3 were waited for; matrix products, arithmetic and copies ran while one was open for 0% of the time, Pallas kernels for 0%

profile of v1, /device:TPU:1, one launch (start us, length us, event | category | flops | bytes accessed | tf_op | source)
XLA Modules:
  0.0 204.4 jit_solution(15572296904792670948)
XLA Ops:
  0.6 0.0 copy-start
  0.6 0.0 copy-start.2
  0.7 1.3 copy.11
  2.0 0.0 copy-done.2
  2.0 0.1 multiply_convert_fusion
  2.1 0.0 copy-done
  2.1 0.3 convolution_bitcast_fusion.1
  2.4 0.7 copy.12
  3.1 15.9 %all-to-all-start = ((f32[32,8,128]{2,1,0:T(8,128)}), f32[32,8,128]{2,1,0:T(8,128)S(1)}, u32[]{:S(2)}, u32[]{:S(2)}) async-start(f32[32,8,128]{2,1,0:T(8,128)} %bitcast.5), calls=%async_computation | async-start | bytes 262144 | tf_op jit(solution)/shard_map/all_to_all | solution.py:15
  19.1 0.0 copy-start.3
  19.1 0.6 copy-done.3
  19.7 0.1 dynamic_slice.6
  19.8 11.4 %all-to-all-done = f32[32,8,128]{2,1,0:T(8,128)S(1)} async-done(((f32[32,8,128]{2,1,0:T(8,128)}), f32[32,8,128]{2,1,0:T(8,128)S(1)}, u32[]{:S(2)}, u32[]{:S(2)}) %all-to-all-start) | async-done | bytes 131104 | tf_op jit(solution)/shard_map/all_to_all | solution.py:15
  31.2 0.1 multiply_convert_fusion.1
  31.3 18.3 %all_to_all.30 = bf16[32,8,128]{2,1,0:T(8,128)(2,1)S(1)} all-to-all(bf16[32,8,128]{2,1,0:T(8,128)(2,1)S(1)} %broadcast_in_dim.7), channel_id=1, replica_groups=mesh['zh'=2,'y'=4,'c'=2,'zl'=8,'x'=4] {'zl','x'}, dimensions={0} | all-to-all | bytes 131072 | tf_op jit(solution)/shard_map/all_to_all | solution.py:21
  49.6 0.3 fusion
  49.9 1.0 copy.13
  50.9 12.7 %all-to-all-start.2 = ((bf16[16,64,256]{2,1,0:T(8,128)(2,1)}), bf16[16,64,256]{2,1,0:T(8,128)(2,1)S(1)}, u32[]{:S(2)}, u32[]{:S(2)}) async-start(bf16[16,64,256]{2,1,0:T(8,128)(2,1)} %bitcast.10), calls=%async_computation.2 | async-start | bytes 1048576 | tf_op jit(solution)/shard_map/all_to_all | solution.py:15
  63.6 0.1 dynamic_slice.7
  63.7 26.1 %all-to-all-done.2 = bf16[16,64,256]{2,1,0:T(8,128)(2,1)S(1)} async-done(((bf16[16,64,256]{2,1,0:T(8,128)(2,1)}), bf16[16,64,256]{2,1,0:T(8,128)(2,1)S(1)}, u32[]{:S(2)}, u32[]{:S(2)}) %all-to-all-start.2) | async-done | bytes 524320 | tf_op jit(solution)/shard_map/all_to_all | solution.py:15
  89.8 0.1 convert_reduce_fusion
  89.9 0.1 broadcast_multiply_fusion
  89.9 0.4 convolution_bitcast_fusion
  90.4 0.2 copy-done.1
  90.6 14.8 %all_to_all.31 = f32[32,8,256]{2,1,0:T(8,128)S(1)} all-to-all(f32[32,8,256]{2,1,0:T(8,128)S(1)} %convolution_bitcast_fusion), channel_id=1, replica_groups=mesh['zh'=2,'y'=4,'c'=2,'zl'=8,'x'=4] {'y','c','x'}, dimensions={0} | all-to-all | bytes 524288 | tf_op jit(solution)/shard_map/all_to_all | solution.py:15
  105.5 21.2 %all_to_all.32 = f32[16,8,256]{2,1,0:T(8,128)S(1)} all-to-all(f32[16,8,256]{2,1,0:T(8,128)S(1)} %broadcast_in_dim.8), channel_id=1, replica_groups=mesh['zh'=2,'y'=4,'c'=2,'zl'=8,'x'=4] {'zh','zl'}, dimensions={0} | all-to-all | bytes 262144 | tf_op jit(solution)/shard_map/all_to_all | solution.py:21
  126.7 0.7 broadcast_in_dim.9
  127.4 6.8 %all-to-all-start.5 = ((f32[32,8,256]{2,1,0:T(8,128)}), f32[32,8,256]{2,1,0:T(8,128)S(1)}, u32[]{:S(2)}, u32[]{:S(2)}) async-start(f32[32,8,256]{2,1,0:T(8,128)} %broadcast_in_dim.9), calls=%async_computation.5 | async-start | bytes 524288 | tf_op jit(solution)/shard_map/all_to_all | solution.py:21
  134.2 0.1 fusion.21
  134.3 8.8 %all-to-all-done.5 = f32[32,8,256]{2,1,0:T(8,128)S(1)} async-done(((f32[32,8,256]{2,1,0:T(8,128)}), f32[32,8,256]{2,1,0:T(8,128)S(1)}, u32[]{:S(2)}, u32[]{:S(2)}) %all-to-all-start.5) | async-done | bytes 262176 | tf_op jit(solution)/shard_map/all_to_all | solution.py:21
  143.0 0.1 copy.14
  143.2 11.7 %cholesky.50 = f32[128,128]{1,0:T(8,128)S(1)} custom-call(f32[128,128]{1,0:T(8,128)S(1)} %cholesky.118), custom_call_target="Cholesky" | custom-call | tf_op jit(solution)/shard_map/jit(cholesky)/cholesky | solution.py:62
  155.0 9.8 %custom-call.15 = f32[1,128,128]{1,2,0:T(8,128)S(1)} custom-call(f32[1,128,128]{2,1,0:T(8,128)S(1)} %get-tuple-element.23), custom_call_target="InvertDiagBlocksLowerTriangular" | custom-call | tf_op jit(solution)/shard_map/jit(cholesky)/cholesky | solution.py:62
  164.8 0.2 constant_dynamic-update-slice_fusion.1
  165.0 0.3 convolution_subtract_fusion
  165.3 11.7 %cholesky.105 = f32[128,128]{1,0:T(8,128)S(1)} custom-call(f32[128,128]{1,0:T(8,128)S(1)} %convolution_subtract_fusion), custom_call_target="Cholesky" | custom-call | tf_op jit(solution)/shard_map/jit(cholesky)/cholesky | solution.py:62
  177.1 0.7 compare_reduce_fusion
  179.1 0.1 triangular_solve.57
  179.1 4.1 %while.1 = (s32[]{:T(128)}, f32[256,256]{1,0:T(8,128)S(1)}, s32[2,2]{1,0:T(2,128)S(1)}, f32[2,128,128]{2,1,0:T(8,128)S(1)}, s32[]{:T(128)}) while((s32[]{:T(128)}, f32[256,256]{1,0:T(8,128)S(1)}, s32[2,2]{1,0:T(2,128)S(1)}, f32[2,128,128]{2,1,0:T(8,128)S(1)}, s32[]{:T(128)}) %tuple.27), condition=%wide.while_cond, body=%wide.while_body.sunk | while | flops 2 | bytes 131181 | solution.py:64
  179.1 0.7 fusion.23
  179.8 1.3 bitcast_dynamic-update-slice_fusion.2
  181.2 0.7 fusion.23
  181.9 1.3 bitcast_dynamic-update-slice_fusion.2
  183.2 19.9 %custom-call.16 = f32[2,128,128]{1,2,0:T(8,128)S(1)} custom-call(f32[2,128,128]{2,1,0:T(8,128)S(1)} %get-tuple-element.9), custom_call_target="InvertDiagBlocksLowerTriangular" | custom-call | tf_op jit(solution)/shard_map/jit(_solve_triangular)/triangular_solve | solution.py:64
  203.1 0.2 fusion.4
  203.3 0.2 convolution_subtract_fusion.1
  203.5 0.2 fusion.3
  203.7 0.6 fusion.7
  (16 shorter events, 0.3 us)
Async XLA Ops:
  0.6 1.4 copy-start
  0.6 1.3 copy-start.2
  3.1 28.0 %all-to-all-start = ((f32[32,8,128]{2,1,0:T(8,128)}), f32[32,8,128]{2,1,0:T(8,128)S(1)}, u32[]{:S(2)}, u32[]{:S(2)}) async-start(f32[32,8,128]{2,1,0:T(8,128)} %bitcast.5), calls=%async_computation | async-start | bytes 262144 | tf_op jit(solution)/shard_map/all_to_all | solution.py:15
  19.1 0.7 copy-start.3
  50.9 38.9 %all-to-all-start.2 = ((bf16[16,64,256]{2,1,0:T(8,128)(2,1)}), bf16[16,64,256]{2,1,0:T(8,128)(2,1)S(1)}, u32[]{:S(2)}, u32[]{:S(2)}) async-start(bf16[16,64,256]{2,1,0:T(8,128)(2,1)} %bitcast.10), calls=%async_computation.2 | async-start | bytes 1048576 | tf_op jit(solution)/shard_map/all_to_all | solution.py:15
  89.9 0.6 copy-start.1
  127.4 15.7 %all-to-all-start.5 = ((f32[32,8,256]{2,1,0:T(8,128)}), f32[32,8,256]{2,1,0:T(8,128)S(1)}, u32[]{:S(2)}, u32[]{:S(2)}) async-start(f32[32,8,256]{2,1,0:T(8,128)} %broadcast_in_dim.9), calls=%async_computation.5 | async-start | bytes 524288 | tf_op jit(solution)/shard_map/all_to_all | solution.py:21

commit v2 on v1

--- a/solution.py
+++ b/solution.py
@@ -1,14 +1,95 @@
+import functools
 import math
 
 import jax
 import jax.numpy as jnp
 from jax import lax
+from jax.experimental import pallas as pl
+from jax.experimental.pallas import tpu as pltpu
 from jax.sharding import Mesh, PartitionSpec as P
 
 OBS_AXES = ("zh", "y", "c")
 FLUX_AXES = ("zl", "x")
 PLANE = ("y", "c", "x")
 LINE = ("zh", "zl")
+HALF = 128
+STEP = 8
+HIGHEST = lax.Precision.HIGHEST
+
+
+def pick(values, index):
+    return jnp.take_along_axis(values, index, axis=1, mode="promise_in_bounds")
+
+
+def eliminate(diag, side, inverse, lanes):
+    sub = lax.broadcasted_iota(jnp.int32, (STEP, HALF), 0)
+    blocks = HALF // STEP
+    for t in range(blocks):
+        top = t * STEP
+        head = diag[top : top + STEP, :]
+        for k in range(STEP):
+            lanes[k * STEP : (k + 1) * STEP, :] = pick(head, jnp.full((STEP, HALF), top + k, jnp.int32))
+        entry = {}
+        for k in range(STEP):
+            for j in range(k, STEP):
+                entry[j, k] = lanes[pl.ds(k * STEP + j, STEP, stride=0), :]
+        rows = [[ref[pl.ds(top + k, STEP, stride=0), :] for ref in (diag, side, inverse)] for k in range(STEP)]
+        for k in range(STEP):
+            scale = lax.rsqrt(entry[k, k])
+            rows[k] = [row * scale for row in rows[k]]
+            mult = {j: entry[j, k] * scale for j in range(k + 1, STEP)}
+            for j in range(k + 1, STEP):
+                for i in range(j, STEP):
+                    entry[i, j] = entry[i, j] - mult[i] * mult[j]
+                rows[j] = [row - mult[j] * pivot for row, pivot in zip(rows[j], rows[k])]
+            for ref, row in zip((side, inverse), rows[k][1:]):
+                ref[top + k : top + k + 1, :] = row[:1, :]
+        for block in range(t + 1, blocks):
+            low = block * STEP
+            index = sub + low
+            work = [ref[low : low + STEP, :] for ref in (diag, side, inverse)]
+            for k in range(STEP):
+                mult = pick(rows[k][0], index)
+                work = [row - mult * pivot for row, pivot in zip(work, rows[k])]
+            for ref, row in zip((diag, side, inverse), work):
+                ref[low : low + STEP, :] = row
+
+
+def identity():
+    shape = (HALF, HALF)
+    return (lax.broadcasted_iota(jnp.int32, shape, 0) == lax.broadcasted_iota(jnp.int32, shape, 1)).astype(jnp.float32)
+
+
+def dot(a, b, dims):
+    return lax.dot_general(a, b, (dims, ((), ())), precision=HIGHEST, preferred_element_type=jnp.float32)
+
+
+def basis_kernel(root, gram, sketch, out, diag, side, low, mixed, high, lanes):
+    diag[...] = gram[:HALF, :HALF]
+    side[...] = gram[:HALF, HALF:]
+    low[...] = identity()
+    eliminate(diag, side, low, lanes)
+    upper = side[...]
+    diag[...] = gram[HALF:, HALF:] - dot(upper, upper, ((0,), (0,)))
+    mixed[...] = -dot(upper, low[...], ((0,), (0,)))
+    high[...] = identity()
+    eliminate(diag, mixed, high, lanes)
+    first, second = sketch[:, :HALF], sketch[:, HALF:]
+    out[:, :HALF] = root * dot(first, low[...], ((1,), (1,)))
+    out[:, HALF:] = root * (dot(first, mixed[...], ((1,), (1,))) + dot(second, high[...], ((1,), (1,))))
+
+
+def basis(gram, sketch, root):
+    square = pltpu.VMEM((HALF, HALF), jnp.float32)
+    vmem = pl.BlockSpec(memory_space=pltpu.VMEM)
+    return pl.pallas_call(
+        functools.partial(basis_kernel, root),
+        out_shape=jax.ShapeDtypeStruct(sketch.shape, jnp.float32),
+        in_specs=[vmem, vmem],
+        out_specs=vmem,
+        scratch_shapes=[square, square, square, square, square, pltpu.VMEM((STEP * STEP, HALF), jnp.float32)],
+        name="cholesky_basis",
+    )(gram, sketch)
 
 
 def scatter_sum(parts, axes):
@@ -59,9 +140,8 @@
     slab = scatter_sum(gram.reshape(lax.axis_size(PLANE), -1, columns), PLANE)
     slab = jnp.sum(gather(slab, LINE), axis=0)
     gram = gather(slab, PLANE).reshape(columns, columns)
-    factor = jnp.linalg.cholesky(gram)
     scale_root = math.sqrt(flux_local * lax.axis_size(FLUX_AXES))
-    basis_out = jax.scipy.linalg.solve_triangular(factor, sketch.T, lower=True).T * scale_root
+    basis_out = basis(gram, sketch, scale_root)
     return (sketch, basis_out)
 
 

time: 205 us -> 152 us (0.74)
  other arithmetic: 55.1 us -> 0.42 us
  blocking collectives: 54.3 us -> 69.9 us
  Pallas kernels: 0 us -> 9.51 us
  waiting for transfers between devices: 46.2 us -> 37.4 us
  starting transfers between devices: 35.4 us -> 28.6 us
  local copies, waits for them, and re-layouts: 9.03 us -> 4.09 us
    another operation x9 -> x0, other arithmetic: 54 us -> none  [the longest x6 34 us: body(): factor = jnp.linalg.cholesky(gram)]
    all_to_all x2 -> x3, blocking collectives: 39.5 us -> 55 us  [gather(): lax.all_to_all(jnp.broadcast_to(piece[None], (count, *piece.shape)), axes...]
    pallas_call x0 -> x1, Pallas kernels: none -> 9.51 us  [basis(): pl.pallas_call(functools.partial(basis_kernel, root), out_shape=jax.Shape...]
    all_to_all x1 -> x0, waiting for transfers between devices: 8.77 us -> none  [gather(): lax.all_to_all(jnp.broadcast_to(piece[None], (count, *piece.shape)), axes...]
    all_to_all x1 -> x0, starting transfers between devices: 6.79 us -> none  [gather(): lax.all_to_all(jnp.broadcast_to(piece[None], (count, *piece.shape)), axes...]
    another operation x9 -> x0, local copies, waits for them, and re-layouts: 4.12 us -> none
  transfers between devices with their start and end apart: 3 -> 2, of which waited for: 3 -> 2; matrix products, arithmetic and copies ran while one was open for 0% -> 0% of each run, Pallas kernels for 0% -> 0%
where the time goes in v2:
time: 152 us
  blocking collectives  69.9 us (46%)
  waiting for transfers between devices  37.4 us (25%)
  starting transfers between devices  28.6 us (19%)
  Pallas kernels  9.51 us (6%)
  local copies, waits for them, and re-layouts  4.09 us (3%)
    all_to_all x3, blocking collectives, gather(): lax.all_to_all(jnp.broadcast_to(piece[None], (count, *piece.shape)), axes...  55 us
    all_to_all x2, waiting for transfers between devices, scatter_sum(): moved = lax.all_to_all(parts, axes, 0, 0, tiled=True)  37.4 us
    all_to_all x2, starting transfers between devices, scatter_sum(): moved = lax.all_to_all(parts, axes, 0, 0, tiled=True)  28.6 us
    all_to_all x1, blocking collectives, scatter_sum(): moved = lax.all_to_all(parts, axes, 0, 0, tiled=True)  14.9 us
    pallas_call x1, Pallas kernels, basis(): pl.pallas_call(functools.partial(basis_kernel, root), out_shape=jax.Shape...  9.51 us
  transfers between devices with their start and end apart: 2, of which 2 were waited for; matrix products, arithmetic and copies ran while one was open for 0% of the time, Pallas kernels for 0%

profile of v2, /device:TPU:1, one launch (start us, length us, event | category | flops | bytes accessed | tf_op | source)
XLA Modules:
  0.0 151.8 jit_solution(15860870409601252671)
XLA Ops:
  0.6 0.0 copy-start
  0.6 0.0 copy-start.2
  0.7 1.3 copy.9
  2.0 0.0 copy-done.2
  2.0 0.1 multiply_convert_fusion
  2.1 0.0 copy-done
  2.1 0.3 convolution_bitcast_fusion.1
  2.4 0.7 copy.10
  3.1 15.9 %all-to-all-start = ((f32[32,8,128]{2,1,0:T(8,128)}), f32[32,8,128]{2,1,0:T(8,128)S(1)}, u32[]{:S(2)}, u32[]{:S(2)}) async-start(f32[32,8,128]{2,1,0:T(8,128)} %bitcast.5), calls=%async_computation | async-start | bytes 262144 | tf_op jit(solution)/shard_map/all_to_all | solution.py:96
  19.1 0.0 copy-start.3
  19.1 0.6 copy-done.3
  19.7 0.1 dynamic_slice.6
  19.8 11.4 %all-to-all-done = f32[32,8,128]{2,1,0:T(8,128)S(1)} async-done(((f32[32,8,128]{2,1,0:T(8,128)}), f32[32,8,128]{2,1,0:T(8,128)S(1)}, u32[]{:S(2)}, u32[]{:S(2)}) %all-to-all-start) | async-done | bytes 131104 | tf_op jit(solution)/shard_map/all_to_all | solution.py:96
  31.2 0.1 multiply_convert_fusion.1
  31.3 18.3 %all_to_all.30 = bf16[32,8,128]{2,1,0:T(8,128)(2,1)S(1)} all-to-all(bf16[32,8,128]{2,1,0:T(8,128)(2,1)S(1)} %broadcast_in_dim.6), channel_id=1, replica_groups=mesh['zh'=2,'y'=4,'c'=2,'zl'=8,'x'=4] {'zl','x'}, dimensions={0} | all-to-all | bytes 131072 | tf_op jit(solution)/shard_map/all_to_all | solution.py:102
  49.6 0.3 fusion
  49.9 1.0 copy.11
  50.9 12.7 %all-to-all-start.2 = ((bf16[16,64,256]{2,1,0:T(8,128)(2,1)}), bf16[16,64,256]{2,1,0:T(8,128)(2,1)S(1)}, u32[]{:S(2)}, u32[]{:S(2)}) async-start(bf16[16,64,256]{2,1,0:T(8,128)(2,1)} %bitcast.10), calls=%async_computation.2 | async-start | bytes 1048576 | tf_op jit(solution)/shard_map/all_to_all | solution.py:96
  63.6 0.1 dynamic_slice.7
  63.7 26.0 %all-to-all-done.2 = bf16[16,64,256]{2,1,0:T(8,128)(2,1)S(1)} async-done(((bf16[16,64,256]{2,1,0:T(8,128)(2,1)}), bf16[16,64,256]{2,1,0:T(8,128)(2,1)S(1)}, u32[]{:S(2)}, u32[]{:S(2)}) %all-to-all-start.2) | async-done | bytes 524320 | tf_op jit(solution)/shard_map/all_to_all | solution.py:96
  89.8 0.1 convert_reduce_fusion
  89.8 0.1 broadcast_multiply_fusion.sketch
  89.9 0.0 copy-start.1
  89.9 0.4 convolution_bitcast_fusion
  90.3 0.2 copy-done.1
  90.5 14.9 %all_to_all.31 = f32[32,8,256]{2,1,0:T(8,128)S(1)} all-to-all(f32[32,8,256]{2,1,0:T(8,128)S(1)} %convolution_bitcast_fusion), channel_id=1, replica_groups=mesh['zh'=2,'y'=4,'c'=2,'zl'=8,'x'=4] {'y','c','x'}, dimensions={0} | all-to-all | bytes 524288 | tf_op jit(solution)/shard_map/all_to_all | solution.py:96
  105.5 21.2 %all_to_all.32 = f32[16,8,256]{2,1,0:T(8,128)S(1)} all-to-all(f32[16,8,256]{2,1,0:T(8,128)S(1)} %broadcast_in_dim.7), channel_id=1, replica_groups=mesh['zh'=2,'y'=4,'c'=2,'zl'=8,'x'=4] {'zh','zl'}, dimensions={0} | all-to-all | bytes 262144 | tf_op jit(solution)/shard_map/all_to_all | solution.py:102
  126.7 15.6 %all_to_all.33 = f32[32,8,256]{2,1,0:T(8,128)} all-to-all(f32[32,8,256]{2,1,0:T(8,128)S(1)} %broadcast_in_dim.8), channel_id=1, replica_groups=mesh['zh'=2,'y'=4,'c'=2,'zl'=8,'x'=4] {'y','c','x'}, dimensions={0} | all-to-all | bytes 524288 | tf_op jit(solution)/shard_map/all_to_all | solution.py:102
  142.3 9.5 %cholesky_basis.1 = f32[64,256]{1,0:T(8,128)} custom-call(f32[256,256]{1,0:T(8,128)} %bitcast.28, f32[64,256]{1,0:T(8,128)} %copy-done.1), custom_call_target="tpu_custom_call" | custom-call | tf_op jit(solution)/shard_map/cholesky_basis/pallas_call | solution.py:85
  (6 shorter events, 0.1 us)
Async XLA Ops:
  0.6 1.4 copy-start
  0.6 1.3 copy-start.2
  3.1 28.0 %all-to-all-start = ((f32[32,8,128]{2,1,0:T(8,128)}), f32[32,8,128]{2,1,0:T(8,128)S(1)}, u32[]{:S(2)}, u32[]{:S(2)}) async-start(f32[32,8,128]{2,1,0:T(8,128)} %bitcast.5), calls=%async_computation | async-start | bytes 262144 | tf_op jit(solution)/shard_map/all_to_all | solution.py:96
  19.1 0.7 copy-start.3
  50.9 38.9 %all-to-all-start.2 = ((bf16[16,64,256]{2,1,0:T(8,128)(2,1)}), bf16[16,64,256]{2,1,0:T(8,128)(2,1)S(1)}, u32[]{:S(2)}, u32[]{:S(2)}) async-start(bf16[16,64,256]{2,1,0:T(8,128)(2,1)} %bitcast.10), calls=%async_computation.2 | async-start | bytes 1048576 | tf_op jit(solution)/shard_map/all_to_all | solution.py:96
  89.9 0.6 copy-start.1

commit v3 on v2

--- a/solution.py
+++ b/solution.py
@@ -10,6 +10,7 @@
 
 OBS_AXES = ("zh", "y", "c")
 FLUX_AXES = ("zl", "x")
+NEAR_OBS = ("y", "c")
 PLANE = ("y", "c", "x")
 LINE = ("zh", "zl")
 HALF = 128
@@ -113,25 +114,34 @@
     return tiles.reshape(rows // 8, cols // 128, 8, 128).transpose(0, 2, 1, 3).reshape(rows, cols)
 
 
+def pull(jacobian, weighted):
+    return lax.dot_general(
+        jacobian, weighted, (((0,), (0,)), ((), ())), preferred_element_type=jnp.float32
+    )
+
+
 def body(jacobian, probes, prior_std, obs_weight):
     block_count, flux_local, probe_count = probes.shape
     obs_local = jacobian.shape[0]
     columns = block_count * probe_count
     obs_parts = lax.axis_size(OBS_AXES)
+    half, far = flux_local // 2, lax.axis_index("zh")
+    near_part = lax.dynamic_slice_in_dim(jacobian, far * half, half, 1)
+    far_part = lax.ppermute(
+        lax.dynamic_slice_in_dim(jacobian, (1 - far) * half, half, 1), "zh", ((0, 1), (1, 0))
+    )
     scaled = (probes.astype(jnp.float32) * prior_std[None, :, None]).astype(jnp.bfloat16)
     stacked = jnp.transpose(scaled, (1, 0, 2)).reshape(flux_local, columns)
     partial = jnp.dot(jacobian, stacked, preferred_element_type=jnp.float32)
     tile = scatter_sum(to_tiles(partial), FLUX_AXES)
     row = lax.axis_index(FLUX_AXES) // (columns // 128) * 8
     weight = lax.dynamic_slice_in_dim(obs_weight, row, 8)
-    weighted = from_tiles(
-        gather((tile * weight[:, None]).astype(jnp.bfloat16), FLUX_AXES), obs_local, columns
-    )
-    adjoint = lax.dot_general(
-        jacobian, weighted, (((0,), (0,)), ((), ())), preferred_element_type=jnp.float32
-    ).astype(jnp.bfloat16)
+    weighted = gather((tile * weight[:, None]).astype(jnp.bfloat16), ("zh",) + FLUX_AXES)
+    weighted = from_tiles(weighted, 2 * obs_local, columns)
+    adjoint = pull(near_part, lax.dynamic_slice_in_dim(weighted, far * obs_local, obs_local))
+    adjoint += pull(far_part, lax.dynamic_slice_in_dim(weighted, (1 - far) * obs_local, obs_local))
     portion = flux_local // obs_parts
-    adjoint = scatter_sum(adjoint.reshape(obs_parts, portion, columns), OBS_AXES)
+    adjoint = scatter_sum(adjoint.astype(jnp.bfloat16).reshape(-1, portion, columns), NEAR_OBS)
     local_std = lax.dynamic_slice_in_dim(prior_std, lax.axis_index(OBS_AXES) * portion, portion)
     sketch = adjoint * local_std[:, None]
     gram = jnp.dot(
@@ -141,8 +151,7 @@
     slab = jnp.sum(gather(slab, LINE), axis=0)
     gram = gather(slab, PLANE).reshape(columns, columns)
     scale_root = math.sqrt(flux_local * lax.axis_size(FLUX_AXES))
-    basis_out = basis(gram, sketch, scale_root)
-    return (sketch, basis_out)
+    return (sketch, basis(gram, sketch, scale_root))
 
 
 def solution(mesh):

time: 152 us -> 142 us (0.934)
  blocking collectives: 69.9 us -> 50.4 us
  starting transfers between devices: 28.6 us -> 43.5 us
  waiting for transfers between devices: 37.4 us -> 31.1 us
    all_to_all x2, waiting for transfers between devices: 37.4 us -> 17.8 us  [scatter_sum(): moved = lax.all_to_all(parts, axes, 0, 0, tiled=True)]
    all_to_all x3 -> x2, blocking collectives: 55 us -> 35.8 us  [gather(): lax.all_to_all(jnp.broadcast_to(piece[None], (count, *piece.shape)), axes...]
    ppermute x0 -> x1, starting transfers between devices: none -> 11.7 us  [body(): lax.ppermute(lax.dynamic_slice_in_dim(jacobian, (1 - far) * half, half, 1...]
    ppermute x0 -> x1, waiting for transfers between devices: none -> 10.1 us  [body(): lax.ppermute(lax.dynamic_slice_in_dim(jacobian, (1 - far) * half, half, 1...]
    all_to_all x0 -> x1, starting transfers between devices: none -> 9.43 us  [gather(): lax.all_to_all(jnp.broadcast_to(piece[None], (count, *piece.shape)), axes...]
    all_to_all x2, starting transfers between devices: 28.6 us -> 22.3 us  [scatter_sum(): moved = lax.all_to_all(parts, axes, 0, 0, tiled=True)]
    all_to_all x0 -> x1, waiting for transfers between devices: none -> 3.22 us  [gather(): lax.all_to_all(jnp.broadcast_to(piece[None], (count, *piece.shape)), axes...]
  transfers between devices with their start and end apart: 2 -> 4, of which waited for: 2 -> 4; matrix products, arithmetic and copies ran while one was open for 0% -> 0% of each run, Pallas kernels for 0% -> 0%
where the time goes in v3:
time: 142 us; the launch traced here: 141 us
  blocking collectives  50.4 us (35%)
  starting transfers between devices  43.5 us (31%)
  waiting for transfers between devices  31.1 us (22%)
  Pallas kernels  9.51 us (7%)
  local copies, waits for them, and re-layouts  3.75 us (3%)
  matrix products  1.9 us (1%)
    all_to_all x2, blocking collectives, gather(): lax.all_to_all(jnp.broadcast_to(piece[None], (count, *piece.shape)), axes...  35.8 us
    all_to_all x2, starting transfers between devices, scatter_sum(): moved = lax.all_to_all(parts, axes, 0, 0, tiled=True)  22.3 us
    all_to_all x2, waiting for transfers between devices, scatter_sum(): moved = lax.all_to_all(parts, axes, 0, 0, tiled=True)  17.8 us
    all_to_all x1, blocking collectives, scatter_sum(): moved = lax.all_to_all(parts, axes, 0, 0, tiled=True)  14.5 us
    ppermute x1, starting transfers between devices, body(): lax.ppermute(lax.dynamic_slice_in_dim(jacobian, (1 - far) * half, half, 1...  11.7 us
    ppermute x1, waiting for transfers between devices, body(): lax.ppermute(lax.dynamic_slice_in_dim(jacobian, (1 - far) * half, half, 1...  10.1 us
    pallas_call x1, Pallas kernels, basis(): pl.pallas_call(functools.partial(basis_kernel, root), out_shape=jax.Shape...  9.51 us
    all_to_all x1, starting transfers between devices, gather(): lax.all_to_all(jnp.broadcast_to(piece[None], (count, *piece.shape)), axes...  9.43 us
  transfers between devices with their start and end apart: 4, of which 4 were waited for; matrix products, arithmetic and copies ran while one was open for 0% of the time, Pallas kernels for 0%

profile of v3, /device:TPU:1, one launch (start us, length us, event | category | flops | bytes accessed | tf_op | source)
XLA Modules:
  0.0 141.3 jit_solution(3905458475478218087)
XLA Ops:
  0.6 0.0 copy-start
  0.6 0.0 copy-start.2
  0.7 1.3 copy.8
  2.0 0.0 copy-done.2
  2.0 0.1 multiply_convert_fusion
  2.1 0.0 copy-done
  2.1 0.3 convolution_bitcast_fusion.1
  2.4 0.7 copy.9
  3.1 15.9 %all-to-all-start = ((f32[32,8,128]{2,1,0:T(8,128)}), f32[32,8,128]{2,1,0:T(8,128)S(1)}, u32[]{:S(2)}, u32[]{:S(2)}) async-start(f32[32,8,128]{2,1,0:T(8,128)} %bitcast.5), calls=%async_computation | async-start | bytes 262144 | tf_op jit(solution)/shard_map/all_to_all | solution.py:97
  19.1 0.0 copy-start.3
  19.1 0.6 copy-done.3
  19.7 0.1 dynamic_slice.19
  19.8 11.4 %all-to-all-done = f32[32,8,128]{2,1,0:T(8,128)S(1)} async-done(((f32[32,8,128]{2,1,0:T(8,128)}), f32[32,8,128]{2,1,0:T(8,128)S(1)}, u32[]{:S(2)}, u32[]{:S(2)}) %all-to-all-start) | async-done | bytes 131104 | tf_op jit(solution)/shard_map/all_to_all | solution.py:97
  31.2 0.1 multiply_convert_fusion.1
  31.3 0.7 broadcast_in_dim.6
  31.9 9.4 %all-to-all-start.1 = ((bf16[64,8,128]{2,1,0:T(8,128)(2,1)}), bf16[64,8,128]{2,1,0:T(8,128)(2,1)S(1)}, u32[]{:S(2)}, u32[]{:S(2)}) async-start(bf16[64,8,128]{2,1,0:T(8,128)(2,1)} %broadcast_in_dim.6), calls=%async_computation.1 | async-start | bytes 262144 | tf_op jit(solution)/shard_map/all_to_all | solution.py:103
  41.4 11.7 %collective-permute-start = (bf16[128,512]{1,0:T(8,128)(2,1)S(1)}, bf16[128,512]{1,0:T(8,128)(2,1)S(1)}, u32[]{:S(2)}, u32[]{:S(2)}) collective-permute-start(bf16[128,512]{1,0:T(8,128)(2,1)S(1)} %constant_dynamic-slice_fusion), channel_id=1, source_target_pairs={{0,256},{256,0},{1,257},{257,1},{2,258},{258,2},{3,259},{259,3},{4... | collective-permute-start | bytes 393224 | tf_op jit(solution)/shard_map/ppermute | solution.py:130
  53.2 3.2 %all-to-all-done.1 = bf16[64,8,128]{2,1,0:T(8,128)(2,1)S(1)} async-done(((bf16[64,8,128]{2,1,0:T(8,128)(2,1)}), bf16[64,8,128]{2,1,0:T(8,128)(2,1)S(1)}, u32[]{:S(2)}, u32[]{:S(2)}) %all-to-all-start.1) | async-done | bytes 131104 | tf_op jit(solution)/shard_map/all_to_all | solution.py:103
  56.4 0.2 fusion.1
  56.6 10.1 %collective-permute-done = bf16[128,512]{1,0:T(8,128)(2,1)S(1)} collective-permute-done((bf16[128,512]{1,0:T(8,128)(2,1)S(1)}, bf16[128,512]{1,0:T(8,128)(2,1)S(1)}, u32[]{:S(2)}, u32[]{:S(2)}) %collective-permute-start) | collective-permute-done | bytes 131104 | tf_op jit(solution)/shard_map/ppermute | solution.py:130
  66.7 0.9 fusion
  67.7 6.4 %all-to-all-start.2 = ((bf16[8,64,256]{2,1,0:T(8,128)(2,1)}), bf16[8,64,256]{2,1,0:T(8,128)(2,1)S(1)}, u32[]{:S(2)}, u32[]{:S(2)}) async-start(bf16[8,64,256]{2,1,0:T(8,128)(2,1)} %bitcast.11), calls=%async_computation.2 | async-start | bytes 524288 | tf_op jit(solution)/shard_map/all_to_all | solution.py:97
  74.1 0.1 dynamic_slice.23
  74.1 6.4 %all-to-all-done.2 = bf16[8,64,256]{2,1,0:T(8,128)(2,1)S(1)} async-done(((bf16[8,64,256]{2,1,0:T(8,128)(2,1)}), bf16[8,64,256]{2,1,0:T(8,128)(2,1)S(1)}, u32[]{:S(2)}, u32[]{:S(2)}) %all-to-all-start.2) | async-done | bytes 262176 | tf_op jit(solution)/shard_map/all_to_all | solution.py:97
  80.6 0.1 broadcast_multiply_fusion.sketch
  80.7 0.0 copy-start.1
  80.7 0.4 convolution_bitcast_fusion
  81.1 0.2 copy-done.1
  81.3 14.5 %all_to_all.30 = f32[32,8,256]{2,1,0:T(8,128)S(1)} all-to-all(f32[32,8,256]{2,1,0:T(8,128)S(1)} %convolution_bitcast_fusion), channel_id=1, replica_groups=mesh['zh'=2,'y'=4,'c'=2,'zl'=8,'x'=4] {'y','c','x'}, dimensions={0} | all-to-all | bytes 524288 | tf_op jit(solution)/shard_map/all_to_all | solution.py:97
  95.9 20.3 %all_to_all.31 = f32[16,8,256]{2,1,0:T(8,128)S(1)} all-to-all(f32[16,8,256]{2,1,0:T(8,128)S(1)} %broadcast_in_dim.7), channel_id=1, replica_groups=mesh['zh'=2,'y'=4,'c'=2,'zl'=8,'x'=4] {'zh','zl'}, dimensions={0} | all-to-all | bytes 262144 | tf_op jit(solution)/shard_map/all_to_all | solution.py:103
  116.2 15.6 %all_to_all.32 = f32[32,8,256]{2,1,0:T(8,128)} all-to-all(f32[32,8,256]{2,1,0:T(8,128)S(1)} %broadcast_in_dim.8), channel_id=1, replica_groups=mesh['zh'=2,'y'=4,'c'=2,'zl'=8,'x'=4] {'y','c','x'}, dimensions={0} | all-to-all | bytes 524288 | tf_op jit(solution)/shard_map/all_to_all | solution.py:103
  131.7 9.5 %cholesky_basis.1 = f32[64,256]{1,0:T(8,128)} custom-call(f32[256,256]{1,0:T(8,128)} %bitcast.25, f32[64,256]{1,0:T(8,128)} %copy-done.1), custom_call_target="tpu_custom_call" | custom-call | tf_op jit(solution)/shard_map/cholesky_basis/pallas_call | solution.py:86
  (7 shorter events, 0.2 us)
Async XLA Ops:
  0.6 1.4 %copy-start = (bf16[128,1024]{1,0:T(8,128)(2,1)S(1)}, bf16[128,1024]{1,0:T(8,128)(2,1)}, u32[]{:S(2)}) copy-start(bf16[128,1024]{1,0:T(8,128)(2,1)} %param.4) | copy-start | bytes 786436
  0.6 1.3 copy-start.2
  3.1 28.0 %all-to-all-start = ((f32[32,8,128]{2,1,0:T(8,128)}), f32[32,8,128]{2,1,0:T(8,128)S(1)}, u32[]{:S(2)}, u32[]{:S(2)}) async-start(f32[32,8,128]{2,1,0:T(8,128)} %bitcast.5), calls=%async_computation | async-start | bytes 262144 | tf_op jit(solution)/shard_map/all_to_all | solution.py:97
  19.1 0.7 copy-start.3
  31.9 24.4 %all-to-all-start.1 = ((bf16[64,8,128]{2,1,0:T(8,128)(2,1)}), bf16[64,8,128]{2,1,0:T(8,128)(2,1)S(1)}, u32[]{:S(2)}, u32[]{:S(2)}) async-start(bf16[64,8,128]{2,1,0:T(8,128)(2,1)} %broadcast_in_dim.6), calls=%async_computation.1 | async-start | bytes 262144 | tf_op jit(solution)/shard_map/all_to_all | solution.py:103
  41.4 25.3 %collective-permute-start = (bf16[128,512]{1,0:T(8,128)(2,1)S(1)}, bf16[128,512]{1,0:T(8,128)(2,1)S(1)}, u32[]{:S(2)}, u32[]{:S(2)}) collective-permute-start(bf16[128,512]{1,0:T(8,128)(2,1)S(1)} %constant_dynamic-slice_fusion), channel_id=1, source_target_pairs={{0,256},{256,0},{1,257},{257,1},{2,258},{258,2},{3,259},{259,3},{4... | collective-permute-start | bytes 393224 | tf_op jit(solution)/shard_map/ppermute | solution.py:130
  67.7 12.8 %all-to-all-start.2 = ((bf16[8,64,256]{2,1,0:T(8,128)(2,1)}), bf16[8,64,256]{2,1,0:T(8,128)(2,1)S(1)}, u32[]{:S(2)}, u32[]{:S(2)}) async-start(bf16[8,64,256]{2,1,0:T(8,128)(2,1)} %bitcast.11), calls=%async_computation.2 | async-start | bytes 524288 | tf_op jit(solution)/shard_map/all_to_all | solution.py:97
  80.7 0.6 copy-start.1

commit v4 on v3

--- a/solution.py
+++ b/solution.py
@@ -124,31 +124,34 @@
     block_count, flux_local, probe_count = probes.shape
     obs_local = jacobian.shape[0]
     columns = block_count * probe_count
-    obs_parts = lax.axis_size(OBS_AXES)
-    half, far = flux_local // 2, lax.axis_index("zh")
-    near_part = lax.dynamic_slice_in_dim(jacobian, far * half, half, 1)
-    far_part = lax.ppermute(
-        lax.dynamic_slice_in_dim(jacobian, (1 - far) * half, half, 1), "zh", ((0, 1), (1, 0))
-    )
+    half, far = flux_local // 2, lax.axis_index("zh").astype(jnp.uint32)
+    rows = (far * obs_local, (1 - far) * obs_local, far * half)
+    portion = flux_local // lax.axis_size(OBS_AXES)
+    local_std = lax.dynamic_slice_in_dim(prior_std, lax.axis_index(OBS_AXES) * portion, portion)
+    row = lax.axis_index(FLUX_AXES) // (columns // 128) * 8
+    weight = lax.dynamic_slice_in_dim(obs_weight, row, 8)
+    sent = lax.dynamic_slice_in_dim(jacobian, (1 - far) * half, half, 1)
     scaled = (probes.astype(jnp.float32) * prior_std[None, :, None]).astype(jnp.bfloat16)
     stacked = jnp.transpose(scaled, (1, 0, 2)).reshape(flux_local, columns)
+    stacked, weight, local_std, sent, rows = lax.optimization_barrier(
+        (stacked, weight, local_std, sent, rows)
+    )
+    near_part = lax.dynamic_slice_in_dim(jacobian, rows[2], half, 1)
+    far_part = lax.ppermute(sent, "zh", ((0, 1), (1, 0)))
     partial = jnp.dot(jacobian, stacked, preferred_element_type=jnp.float32)
-    tile = scatter_sum(to_tiles(partial), FLUX_AXES)
-    row = lax.axis_index(FLUX_AXES) // (columns // 128) * 8
-    weight = lax.dynamic_slice_in_dim(obs_weight, row, 8)
+    moved = lax.all_to_all(to_tiles(partial), FLUX_AXES, 0, 0, tiled=True)
+    tile = jnp.sum(moved, axis=0)
     weighted = gather((tile * weight[:, None]).astype(jnp.bfloat16), ("zh",) + FLUX_AXES)
     weighted = from_tiles(weighted, 2 * obs_local, columns)
-    adjoint = pull(near_part, lax.dynamic_slice_in_dim(weighted, far * obs_local, obs_local))
-    adjoint += pull(far_part, lax.dynamic_slice_in_dim(weighted, (1 - far) * obs_local, obs_local))
-    portion = flux_local // obs_parts
+    adjoint = pull(near_part, lax.dynamic_slice_in_dim(weighted, rows[0], obs_local))
+    adjoint += pull(far_part, lax.dynamic_slice_in_dim(weighted, rows[1], obs_local))
     adjoint = scatter_sum(adjoint.astype(jnp.bfloat16).reshape(-1, portion, columns), NEAR_OBS)
-    local_std = lax.dynamic_slice_in_dim(prior_std, lax.axis_index(OBS_AXES) * portion, portion)
     sketch = adjoint * local_std[:, None]
     gram = jnp.dot(
         sketch.T, sketch, precision=lax.Precision.HIGHEST, preferred_element_type=jnp.float32
     )
     slab = scatter_sum(gram.reshape(lax.axis_size(PLANE), -1, columns), PLANE)
-    slab = jnp.sum(gather(slab, LINE), axis=0)
+    slab = jnp.sum(gather(slab.astype(jnp.bfloat16), LINE).astype(jnp.float32), axis=0)
     gram = gather(slab, PLANE).reshape(columns, columns)
     scale_root = math.sqrt(flux_local * lax.axis_size(FLUX_AXES))
     return (sketch, basis(gram, sketch, scale_root))
@@ -158,6 +161,5 @@
     split = Mesh(mesh.devices.reshape(2, 4, 2, 8, 4), ("zh", "y", "c", "zl", "x"))
     in_specs = (P(OBS_AXES, FLUX_AXES), P(None, FLUX_AXES, None), P(FLUX_AXES), P(OBS_AXES))
     out_specs = (P(FLUX_AXES + OBS_AXES, None), P(FLUX_AXES + OBS_AXES, None))
-    return jax.shard_map(
-        body, mesh=split, in_specs=in_specs, out_specs=out_specs, check_vma=False
-    )
+
+    return jax.shard_map(body, mesh=split, in_specs=in_specs, out_specs=out_specs, check_vma=False)

time: 142 us -> 139 us (0.979)
  blocking collectives: 50.4 us -> 89.1 us
  starting transfers between devices: 43.5 us -> 21.2 us
  waiting for transfers between devices: 31.1 us -> 13.3 us
    all_to_all x0 -> x1, blocking collectives: none -> 27.8 us  [body(): moved = lax.all_to_all(to_tiles(partial), FLUX_AXES, 0, 0, tiled=True)]
    all_to_all x2 -> x0, starting transfers between devices: 22.3 us -> none  [scatter_sum(): moved = lax.all_to_all(parts, axes, 0, 0, tiled=True)]
    all_to_all x2 -> x0, waiting for transfers between devices: 17.8 us -> none  [scatter_sum(): moved = lax.all_to_all(parts, axes, 0, 0, tiled=True)]
    all_to_all x1 -> x2, blocking collectives: 14.5 us -> 27.1 us  [scatter_sum(): moved = lax.all_to_all(parts, axes, 0, 0, tiled=True)]
    all_to_all x2, blocking collectives: 35.8 us -> 34.2 us  [gather(): lax.all_to_all(jnp.broadcast_to(piece[None], (count, *piece.shape)), axes...]
  transfers between devices with their start and end apart: 4 -> 2, of which waited for: 4 -> 2; matrix products, arithmetic and copies ran while one was open for 0% -> 0% of each run, Pallas kernels for 0% -> 0%
where the time goes in v4:
time: 139 us
  blocking collectives  89.1 us (64%)
  starting transfers between devices  21.2 us (15%)
  waiting for transfers between devices  13.3 us (10%)
  Pallas kernels  9.5 us (7%)
  local copies, waits for them, and re-layouts  3.09 us (2%)
    all_to_all x2, blocking collectives, gather(): lax.all_to_all(jnp.broadcast_to(piece[None], (count, *piece.shape)), axes...  34.2 us
    all_to_all x1, blocking collectives, body(): moved = lax.all_to_all(to_tiles(partial), FLUX_AXES, 0, 0, tiled=True)  27.8 us
    all_to_all x2, blocking collectives, scatter_sum(): moved = lax.all_to_all(parts, axes, 0, 0, tiled=True)  27.1 us
    ppermute x1, starting transfers between devices, body(): far_part = lax.ppermute(sent, 'zh', ((0, 1), (1, 0)))  11.7 us
    ppermute x1, waiting for transfers between devices, body(): far_part = lax.ppermute(sent, 'zh', ((0, 1), (1, 0)))  10.1 us
    pallas_call x1, Pallas kernels, basis(): pl.pallas_call(functools.partial(basis_kernel, root), out_shape=jax.Shape...  9.5 us
    all_to_all x1, starting transfers between devices, gather(): lax.all_to_all(jnp.broadcast_to(piece[None], (count, *piece.shape)), axes...  9.43 us
    all_to_all x1, waiting for transfers between devices, gather(): lax.all_to_all(jnp.broadcast_to(piece[None], (count, *piece.shape)), axes...  3.25 us
  transfers between devices with their start and end apart: 2, of which 2 were waited for; matrix products, arithmetic and copies ran while one was open for 0% of the time, Pallas kernels for 0%

profile of v4, /device:TPU:1, one launch (start us, length us, event | category | flops | bytes accessed | tf_op | source)
XLA Modules:
  0.0 138.7 jit_solution(3865660614580927666)
XLA Ops:
  0.6 0.0 copy-start
  0.7 0.0 copy-start.2
  0.7 1.3 copy.8
  2.0 0.0 copy-done.2
  2.0 0.1 dynamic_slice.19
  2.1 0.1 multiply_convert_fusion
  2.2 0.0 copy-start.3
  2.2 0.6 copy-done.3
  2.8 0.1 dynamic_slice.18
  2.9 0.0 copy-done
  2.9 0.3 convolution_bitcast_fusion.1
  3.2 0.1 copy.9
  3.3 27.8 %all_to_all.30 = f32[32,8,128]{2,1,0:T(8,128)S(1)} all-to-all(f32[32,8,128]{2,1,0:T(8,128)S(1)} %bitcast.27), channel_id=1, replica_groups=mesh['zh'=2,'y'=4,'c'=2,'zl'=8,'x'=4] {'zl','x'}, dimensions={0} | all-to-all | bytes 262144 | tf_op jit(solution)/shard_map/all_to_all | solution.py:142
  31.2 0.1 multiply_convert_fusion.1
  31.3 0.7 broadcast_in_dim.6
  31.9 9.4 %all-to-all-start.1 = ((bf16[64,8,128]{2,1,0:T(8,128)(2,1)}), bf16[64,8,128]{2,1,0:T(8,128)(2,1)S(1)}, u32[]{:S(2)}, u32[]{:S(2)}) async-start(bf16[64,8,128]{2,1,0:T(8,128)(2,1)} %broadcast_in_dim.6), calls=%async_computation.1 | async-start | bytes 262144 | tf_op jit(solution)/shard_map/all_to_all | solution.py:103
  41.4 11.7 %collective-permute-start = (bf16[128,512]{1,0:T(8,128)(2,1)S(1)}, bf16[128,512]{1,0:T(8,128)(2,1)S(1)}, u32[]{:S(2)}, u32[]{:S(2)}) collective-permute-start(bf16[128,512]{1,0:T(8,128)(2,1)S(1)} %constant_dynamic-slice_fusion), channel_id=1, source_target_pairs={{0,256},{256,0},{1,257},{257,1},{2,258},{258,2},{3,259},{259,3},{4... | collective-permute-start | bytes 393224 | tf_op jit(solution)/shard_map/ppermute | solution.py:140
  53.1 3.3 %all-to-all-done.1 = bf16[64,8,128]{2,1,0:T(8,128)(2,1)S(1)} async-done(((bf16[64,8,128]{2,1,0:T(8,128)(2,1)}), bf16[64,8,128]{2,1,0:T(8,128)(2,1)S(1)}, u32[]{:S(2)}, u32[]{:S(2)}) %all-to-all-start.1) | async-done | bytes 131104 | tf_op jit(solution)/shard_map/all_to_all | solution.py:103
  56.4 0.3 fusion.1
  56.7 10.1 %collective-permute-done = bf16[128,512]{1,0:T(8,128)(2,1)S(1)} collective-permute-done((bf16[128,512]{1,0:T(8,128)(2,1)S(1)}, bf16[128,512]{1,0:T(8,128)(2,1)S(1)}, u32[]{:S(2)}, u32[]{:S(2)}) %collective-permute-start) | collective-permute-done | bytes 131104 | tf_op jit(solution)/shard_map/ppermute | solution.py:140
  66.8 0.3 fusion
  67.0 12.6 %all_to_all.31 = bf16[8,64,256]{2,1,0:T(8,128)(2,1)S(1)} all-to-all(bf16[8,64,256]{2,1,0:T(8,128)(2,1)S(1)} %bitcast.25), channel_id=1, replica_groups=mesh['zh'=2,'y'=4,'c'=2,'zl'=8,'x'=4] {'y','c'}, dimensions={0} | all-to-all | bytes 524288 | tf_op jit(solution)/shard_map/all_to_all | solution.py:97
  79.7 0.1 broadcast_multiply_fusion.sketch
  79.7 0.0 copy-start.1
  79.8 0.4 convolution_bitcast_fusion
  80.2 0.2 copy-done.1
  80.4 14.5 %all_to_all.32 = f32[32,8,256]{2,1,0:T(8,128)S(1)} all-to-all(f32[32,8,256]{2,1,0:T(8,128)S(1)} %convolution_bitcast_fusion), channel_id=1, replica_groups=mesh['zh'=2,'y'=4,'c'=2,'zl'=8,'x'=4] {'y','c','x'}, dimensions={0} | all-to-all | bytes 524288 | tf_op jit(solution)/shard_map/all_to_all | solution.py:97
  95.0 19.7 %all_to_all.33 = bf16[16,8,256]{2,1,0:T(8,128)(2,1)S(1)} all-to-all(bf16[16,8,256]{2,1,0:T(8,128)(2,1)S(1)} %broadcast_in_dim.7), channel_id=1, replica_groups=mesh['zh'=2,'y'=4,'c'=2,'zl'=8,'x'=4] {'zh','zl'}, dimensions={0} | all-to-all | bytes 131072 | tf_op jit(solution)/shard_map/all_to_all | solution.py:103
  114.7 14.5 %all_to_all.34 = f32[32,8,256]{2,1,0:T(8,128)} all-to-all(f32[32,8,256]{2,1,0:T(8,128)S(1)} %broadcast_in_dim.8), channel_id=1, replica_groups=mesh['zh'=2,'y'=4,'c'=2,'zl'=8,'x'=4] {'y','c','x'}, dimensions={0} | all-to-all | bytes 524288 | tf_op jit(solution)/shard_map/all_to_all | solution.py:103
  129.2 9.5 %cholesky_basis.1 = f32[64,256]{1,0:T(8,128)} custom-call(f32[256,256]{1,0:T(8,128)} %bitcast.26, f32[64,256]{1,0:T(8,128)} %copy-done.1), custom_call_target="tpu_custom_call" | custom-call | tf_op jit(solution)/shard_map/cholesky_basis/pallas_call | solution.py:86
  (7 shorter events, 0.2 us)
Async XLA Ops:
  0.6 2.3 %copy-start = (bf16[128,1024]{1,0:T(8,128)(2,1)S(1)}, bf16[128,1024]{1,0:T(8,128)(2,1)}, u32[]{:S(2)}) copy-start(bf16[128,1024]{1,0:T(8,128)(2,1)} %param.4) | copy-start | bytes 786436
  0.7 1.3 copy-start.2
  2.2 0.7 copy-start.3
  31.9 24.4 %all-to-all-start.1 = ((bf16[64,8,128]{2,1,0:T(8,128)(2,1)}), bf16[64,8,128]{2,1,0:T(8,128)(2,1)S(1)}, u32[]{:S(2)}, u32[]{:S(2)}) async-start(bf16[64,8,128]{2,1,0:T(8,128)(2,1)} %broadcast_in_dim.6), calls=%async_computation.1 | async-start | bytes 262144 | tf_op jit(solution)/shard_map/all_to_all | solution.py:103
  41.4 25.4 %collective-permute-start = (bf16[128,512]{1,0:T(8,128)(2,1)S(1)}, bf16[128,512]{1,0:T(8,128)(2,1)S(1)}, u32[]{:S(2)}, u32[]{:S(2)}) collective-permute-start(bf16[128,512]{1,0:T(8,128)(2,1)S(1)} %constant_dynamic-slice_fusion), channel_id=1, source_target_pairs={{0,256},{256,0},{1,257},{257,1},{2,258},{258,2},{3,259},{259,3},{4... | collective-permute-start | bytes 393224 | tf_op jit(solution)/shard_map/ppermute | solution.py:140
  79.7 0.6 copy-start.1

commit v5 on v4

--- a/solution.py
+++ b/solution.py
@@ -93,6 +93,36 @@
     )(gram, sketch)
 
 
+def forward_kernel(jacobian, probes, spread, out, stacked):
+    sub = lax.broadcasted_iota(jnp.int32, (STEP, HALF), 0)
+    blocks, flux_local, _ = probes.shape
+    pair = 2 * STEP
+    for low in range(0, flux_local, pair):
+        row = spread[pl.ds(low // HALF, STEP, stride=0), :]
+        factor = jnp.concatenate([pick(row, sub + (low + half) % HALF) for half in (0, STEP)], axis=0)
+        for b in range(blocks):
+            scaled = probes[b, low : low + pair, :].astype(jnp.float32) * factor
+            stacked[low : low + pair, b * HALF : (b + 1) * HALF] = scaled.astype(jnp.bfloat16)
+    total = jnp.dot(jacobian[...], stacked[...], preferred_element_type=jnp.float32)
+    for k in range(out.shape[0]):
+        r, c = k // blocks * STEP, k % blocks * HALF
+        out[k] = total[r : r + STEP, c : c + HALF]
+
+
+def forward_tiles(jacobian, probes, prior_std):
+    rows, flux_local = jacobian.shape
+    columns = probes.shape[0] * probes.shape[2]
+    vmem = pl.BlockSpec(memory_space=pltpu.VMEM)
+    return pl.pallas_call(
+        forward_kernel,
+        out_shape=jax.ShapeDtypeStruct((rows * columns // (STEP * HALF), STEP, HALF), jnp.float32),
+        in_specs=[vmem, vmem, vmem],
+        out_specs=vmem,
+        scratch_shapes=[pltpu.VMEM((flux_local, columns), jnp.bfloat16)],
+        name="forward_tiles",
+    )(jacobian, probes, prior_std.reshape(flux_local // HALF, HALF))
+
+
 def scatter_sum(parts, axes):
     moved = lax.all_to_all(parts, axes, 0, 0, tiled=True)
     return jnp.sum(moved.astype(jnp.float32), axis=0)
@@ -103,11 +133,6 @@
     return lax.all_to_all(
         jnp.broadcast_to(piece[None], (count, *piece.shape)), axes, 0, 0, tiled=True
     )
-
-
-def to_tiles(full):
-    rows, cols = full.shape
-    return full.reshape(rows // 8, 8, cols // 128, 128).transpose(0, 2, 1, 3).reshape(-1, 8, 128)
 
 
 def from_tiles(tiles, rows, cols):
@@ -121,9 +146,9 @@
 
 
 def body(jacobian, probes, prior_std, obs_weight):
-    block_count, flux_local, probe_count = probes.shape
+    flux_local = probes.shape[1]
     obs_local = jacobian.shape[0]
-    columns = block_count * probe_count
+    columns = probes.shape[0] * probes.shape[2]
     half, far = flux_local // 2, lax.axis_index("zh").astype(jnp.uint32)
     rows = (far * obs_local, (1 - far) * obs_local, far * half)
     portion = flux_local // lax.axis_size(OBS_AXES)
@@ -131,16 +156,12 @@
     row = lax.axis_index(FLUX_AXES) // (columns // 128) * 8
     weight = lax.dynamic_slice_in_dim(obs_weight, row, 8)
     sent = lax.dynamic_slice_in_dim(jacobian, (1 - far) * half, half, 1)
-    scaled = (probes.astype(jnp.float32) * prior_std[None, :, None]).astype(jnp.bfloat16)
-    stacked = jnp.transpose(scaled, (1, 0, 2)).reshape(flux_local, columns)
-    stacked, weight, local_std, sent, rows = lax.optimization_barrier(
-        (stacked, weight, local_std, sent, rows)
-    )
+    far_part = lax.ppermute(sent, "zh", ((0, 1), (1, 0)))
+    tiles = forward_tiles(jacobian, probes, prior_std)
+    moved = lax.all_to_all(tiles, FLUX_AXES, 0, 0, tiled=True)
+    tile = jnp.sum(moved, axis=0)
+    tile, weight, local_std, rows = lax.optimization_barrier((tile, weight, local_std, rows))
     near_part = lax.dynamic_slice_in_dim(jacobian, rows[2], half, 1)
-    far_part = lax.ppermute(sent, "zh", ((0, 1), (1, 0)))
-    partial = jnp.dot(jacobian, stacked, preferred_element_type=jnp.float32)
-    moved = lax.all_to_all(to_tiles(partial), FLUX_AXES, 0, 0, tiled=True)
-    tile = jnp.sum(moved, axis=0)
     weighted = gather((tile * weight[:, None]).astype(jnp.bfloat16), ("zh",) + FLUX_AXES)
     weighted = from_tiles(weighted, 2 * obs_local, columns)
     adjoint = pull(near_part, lax.dynamic_slice_in_dim(weighted, rows[0], obs_local))
@@ -150,8 +171,9 @@
     gram = jnp.dot(
         sketch.T, sketch, precision=lax.Precision.HIGHEST, preferred_element_type=jnp.float32
     )
-    slab = scatter_sum(gram.reshape(lax.axis_size(PLANE), -1, columns), PLANE)
-    slab = jnp.sum(gather(slab.astype(jnp.bfloat16), LINE).astype(jnp.float32), axis=0)
+    slab = scatter_sum(gram.astype(jnp.bfloat16).reshape(lax.axis_size(PLANE), -1, columns), PLANE)
+    slab = lax.optimization_barrier(slab).astype(jnp.bfloat16)
+    slab = jnp.sum(gather(slab, LINE).astype(jnp.float32), axis=0)
     gram = gather(slab, PLANE).reshape(columns, columns)
     scale_root = math.sqrt(flux_local * lax.axis_size(FLUX_AXES))
     return (sketch, basis(gram, sketch, scale_root))

time: 139 us -> 138 us (level)
  blocking collectives: 89.1 us -> 60 us
  starting transfers between devices: 21.2 us -> 37.1 us
  waiting for transfers between devices: 13.3 us -> 23.9 us
  Pallas kernels: 9.5 us -> 11.9 us
    all_to_all x1 -> x0, blocking collectives: 27.8 us -> none  [body(): moved = lax.all_to_all(to_tiles(partial), FLUX_AXES, 0, 0, tiled=True)]
    all_to_all x0 -> x1, starting transfers between devices: none -> 15.9 us  [body(): moved = lax.all_to_all(tiles, FLUX_AXES, 0, 0, tiled=True)]
    all_to_all x0 -> x1, waiting for transfers between devices: none -> 10.6 us  [body(): moved = lax.all_to_all(tiles, FLUX_AXES, 0, 0, tiled=True)]
    pallas_call x0 -> x1, Pallas kernels: none -> 2.38 us  [forward_tiles(): pl.pallas_call(forward_kernel, out_shape=jax.ShapeDtypeStruct((rows * col...]
  transfers between devices with their start and end apart: 2 -> 3, of which waited for: 2 -> 3; matrix products, arithmetic and copies ran while one was open for 0% -> 1% of each run, Pallas kernels for 0% -> 0%
where the time goes in v5:
time: 138 us; the launch traced here: 137 us
  blocking collectives  60 us (43%)
  starting transfers between devices  37.1 us (27%)
  waiting for transfers between devices  23.9 us (17%)
  Pallas kernels  11.9 us (9%)
  local copies, waits for them, and re-layouts  2.4 us (2%)
    all_to_all x2, blocking collectives, gather(): lax.all_to_all(jnp.broadcast_to(piece[None], (count, *piece.shape)), axes...  34.2 us
    all_to_all x2, blocking collectives, scatter_sum(): moved = lax.all_to_all(parts, axes, 0, 0, tiled=True)  25.9 us
    all_to_all x1, starting transfers between devices, body(): moved = lax.all_to_all(tiles, FLUX_AXES, 0, 0, tiled=True)  15.9 us
    ppermute x1, starting transfers between devices, body(): far_part = lax.ppermute(sent, 'zh', ((0, 1), (1, 0)))  11.7 us
    all_to_all x1, waiting for transfers between devices, body(): moved = lax.all_to_all(tiles, FLUX_AXES, 0, 0, tiled=True)  10.6 us
    ppermute x1, waiting for transfers between devices, body(): far_part = lax.ppermute(sent, 'zh', ((0, 1), (1, 0)))  10 us
    pallas_call x1, Pallas kernels, basis(): pl.pallas_call(functools.partial(basis_kernel, root), out_shape=jax.Shape...  9.51 us
    all_to_all x1, starting transfers between devices, gather(): lax.all_to_all(jnp.broadcast_to(piece[None], (count, *piece.shape)), axes...  9.43 us
  transfers between devices with their start and end apart: 3, of which 3 were waited for; matrix products, arithmetic and copies ran while one was open for 1% of the time, Pallas kernels for 0%

profile of v5, /device:TPU:1, one launch (start us, length us, event | category | flops | bytes accessed | tf_op | source)
XLA Modules:
  0.0 137.3 jit_solution(9191376647598438839)
XLA Ops:
  0.6 2.4 %forward_tiles.1 = f32[32,8,128]{2,1,0:T(8,128)} custom-call(bf16[128,1024]{1,0:T(8,128)(2,1)} %jacobian.1, bf16[2,1024,128]{2,1,0:T(8,128)(2,1)} %probes.1, f32[8,128]{1,0:T(8,128)} %bitcast.17), custom_call_target="tpu_custom_call" | custom-call | tf_op jit(solution)/shard_map/forward_tiles/pallas_call | solution.py:116
  3.0 15.9 %all-to-all-start = ((f32[32,8,128]{2,1,0:T(8,128)}), f32[32,8,128]{2,1,0:T(8,128)S(1)}, u32[]{:S(2)}, u32[]{:S(2)}) async-start(f32[32,8,128]{2,1,0:T(8,128)} %forward_tiles.1), calls=%async_computation | async-start | bytes 262144 | tf_op jit(solution)/shard_map/all_to_all | solution.py:161
  19.0 0.8 dynamic_slice.19
  19.7 0.0 copy-start.2
  19.7 0.7 copy-done.2
  20.4 0.1 dynamic_slice.18
  20.4 0.0 copy-start
  20.4 10.6 %all-to-all-done = f32[32,8,128]{2,1,0:T(8,128)S(1)} async-done(((f32[32,8,128]{2,1,0:T(8,128)}), f32[32,8,128]{2,1,0:T(8,128)S(1)}, u32[]{:S(2)}, u32[]{:S(2)}) %all-to-all-start) | async-done | bytes 131104 | tf_op jit(solution)/shard_map/all_to_all | solution.py:161
  31.1 0.1 multiply_convert_fusion
  31.2 0.7 broadcast_in_dim.6
  31.8 9.4 %all-to-all-start.1 = ((bf16[64,8,128]{2,1,0:T(8,128)(2,1)}), bf16[64,8,128]{2,1,0:T(8,128)(2,1)S(1)}, u32[]{:S(2)}, u32[]{:S(2)}) async-start(bf16[64,8,128]{2,1,0:T(8,128)(2,1)} %broadcast_in_dim.6), calls=%async_computation.1 | async-start | bytes 262144 | tf_op jit(solution)/shard_map/all_to_all | solution.py:133
  41.3 0.0 copy-done
  41.3 11.7 %collective-permute-start = (bf16[128,512]{1,0:T(8,128)(2,1)S(1)}, bf16[128,512]{1,0:T(8,128)(2,1)S(1)}, u32[]{:S(2)}, u32[]{:S(2)}) collective-permute-start(bf16[128,512]{1,0:T(8,128)(2,1)S(1)} %constant_dynamic-slice_fusion), channel_id=1, source_target_pairs={{0,256},{256,0},{1,257},{257,1},{2,258},{258,2},{3,259},{259,3},{4... | collective-permute-start | bytes 393224 | tf_op jit(solution)/shard_map/ppermute | solution.py:159
  53.0 3.2 %all-to-all-done.1 = bf16[64,8,128]{2,1,0:T(8,128)(2,1)S(1)} async-done(((bf16[64,8,128]{2,1,0:T(8,128)(2,1)}), bf16[64,8,128]{2,1,0:T(8,128)(2,1)S(1)}, u32[]{:S(2)}, u32[]{:S(2)}) %all-to-all-start.1) | async-done | bytes 131104 | tf_op jit(solution)/shard_map/all_to_all | solution.py:133
  56.3 0.3 fusion.2
  56.6 10.0 %collective-permute-done = bf16[128,512]{1,0:T(8,128)(2,1)S(1)} collective-permute-done((bf16[128,512]{1,0:T(8,128)(2,1)S(1)}, bf16[128,512]{1,0:T(8,128)(2,1)S(1)}, u32[]{:S(2)}, u32[]{:S(2)}) %collective-permute-start) | collective-permute-done | bytes 131104 | tf_op jit(solution)/shard_map/ppermute | solution.py:159
  66.6 0.2 fusion
  66.9 12.6 %all_to_all.30 = bf16[8,64,256]{2,1,0:T(8,128)(2,1)S(1)} all-to-all(bf16[8,64,256]{2,1,0:T(8,128)(2,1)S(1)} %bitcast.13), channel_id=1, replica_groups=mesh['zh'=2,'y'=4,'c'=2,'zl'=8,'x'=4] {'y','c'}, dimensions={0} | all-to-all | bytes 524288 | tf_op jit(solution)/shard_map/all_to_all | solution.py:127
  79.5 0.1 broadcast_multiply_fusion.sketch
  79.6 0.0 copy-start.1
  79.6 0.4 fusion.1
  80.0 0.2 copy-done.1
  80.2 13.3 %all_to_all.31 = bf16[32,8,256]{2,1,0:T(8,128)(2,1)S(1)} all-to-all(bf16[32,8,256]{2,1,0:T(8,128)(2,1)S(1)} %fusion.1), channel_id=1, replica_groups=mesh['zh'=2,'y'=4,'c'=2,'zl'=8,'x'=4] {'y','c','x'}, dimensions={0} | all-to-all | bytes 262144 | tf_op jit(solution)/shard_map/all_to_all | solution.py:127
  93.6 19.7 %all_to_all.32 = bf16[16,8,256]{2,1,0:T(8,128)(2,1)S(1)} all-to-all(bf16[16,8,256]{2,1,0:T(8,128)(2,1)S(1)} %broadcast_in_dim.7), channel_id=1, replica_groups=mesh['zh'=2,'y'=4,'c'=2,'zl'=8,'x'=4] {'zh','zl'}, dimensions={0} | all-to-all | bytes 131072 | tf_op jit(solution)/shard_map/all_to_all | solution.py:133
  113.3 14.4 %all_to_all.33 = f32[32,8,256]{2,1,0:T(8,128)} all-to-all(f32[32,8,256]{2,1,0:T(8,128)S(1)} %broadcast_in_dim.8), channel_id=1, replica_groups=mesh['zh'=2,'y'=4,'c'=2,'zl'=8,'x'=4] {'y','c','x'}, dimensions={0} | all-to-all | bytes 524288 | tf_op jit(solution)/shard_map/all_to_all | solution.py:133
  127.8 9.5 %cholesky_basis.1 = f32[64,256]{1,0:T(8,128)} custom-call(f32[256,256]{1,0:T(8,128)} %bitcast.14, f32[64,256]{1,0:T(8,128)} %copy-done.1), custom_call_target="tpu_custom_call" | custom-call | tf_op jit(solution)/shard_map/cholesky_basis/pallas_call | solution.py:86
  (7 shorter events, 0.2 us)
Async XLA Ops:
  3.0 28.0 %all-to-all-start = ((f32[32,8,128]{2,1,0:T(8,128)}), f32[32,8,128]{2,1,0:T(8,128)S(1)}, u32[]{:S(2)}, u32[]{:S(2)}) async-start(f32[32,8,128]{2,1,0:T(8,128)} %forward_tiles.1), calls=%async_computation | async-start | bytes 262144 | tf_op jit(solution)/shard_map/all_to_all | solution.py:161
  19.7 0.7 copy-start.2
  20.4 20.8 %copy-start = (bf16[128,1024]{1,0:T(8,128)(2,1)S(1)}, bf16[128,1024]{1,0:T(8,128)(2,1)}, u32[]{:S(2)}) copy-start(bf16[128,1024]{1,0:T(8,128)(2,1)} %jacobian.1) | copy-start | bytes 786436
  31.8 24.4 %all-to-all-start.1 = ((bf16[64,8,128]{2,1,0:T(8,128)(2,1)}), bf16[64,8,128]{2,1,0:T(8,128)(2,1)S(1)}, u32[]{:S(2)}, u32[]{:S(2)}) async-start(bf16[64,8,128]{2,1,0:T(8,128)(2,1)} %broadcast_in_dim.6), calls=%async_computation.1 | async-start | bytes 262144 | tf_op jit(solution)/shard_map/all_to_all | solution.py:133
  41.3 25.3 %collective-permute-start = (bf16[128,512]{1,0:T(8,128)(2,1)S(1)}, bf16[128,512]{1,0:T(8,128)(2,1)S(1)}, u32[]{:S(2)}, u32[]{:S(2)}) collective-permute-start(bf16[128,512]{1,0:T(8,128)(2,1)S(1)} %constant_dynamic-slice_fusion), channel_id=1, source_target_pairs={{0,256},{256,0},{1,257},{257,1},{2,258},{258,2},{3,259},{259,3},{4... | collective-permute-start | bytes 393224 | tf_op jit(solution)/shard_map/ppermute | solution.py:159
  79.6 0.6 copy-start.1
